TPU v7x, 128 devices: a whole 4x4x4 slice. The times are simulated.
128 devices in a mesh: head: 16 (over z, y), batch: 8 (over x, core).
Axes of the slice: x: 4, y: 4, z: 4, core: 2. Of those that a mesh axis runs over, the one named last changes fastest.
Arguments:
- incoming_hidden_stream: bfloat16 [1024, 4096], P('batch'), may hold values from -6 to 6
- reception_projection: bfloat16 [4096, 4096], P(None, 'head'), may hold values from -0.09375 to 0.09375
- address_projection: bfloat16 [4096, 4096], P(None, 'head'), may hold values from -0.09375 to 0.09375
- payload_projection: bfloat16 [4096, 4096], P(None, 'head'), may hold values from -0.09375 to 0.09375
- sigmoid_filter_matrix: bfloat16 [4096, 4096], P(None, 'head'), may hold values from -0.09375 to 0.09375
- forgetting_speed: float32 [1024, 4096], P('batch', 'head'), may hold values from 0.01 to 1.5
- adaptation_step_size: float32 [1024, 4096], P('batch', 'head'), may hold values from 0 to 1
- diagonal_boost: float32 [4096], P('head'), may hold values from -0.6 to 0.6
- subspace_standardize_scale: float32 [4096], P('head'), may hold values from 0.5 to 2
- recurrent_memory_matrix: float32 [128, 64, 64, 64], P('batch', 'head'), may hold values from -6 to 6
- emission_projection: bfloat16 [4096, 4096], P('head'), may hold values from -0.09375 to 0.09375
- closing_standardize_scale: float32 [4096], replicated, may hold values from 0.7 to 2
- lexicon_projection: bfloat16 [4096, 65536], P(None, ('head', 'batch')), may hold values from -32 to 32
- proposed_tokens_list: int32 [128, 8], P('batch'), may hold values from 0 to 65535
- threshold_milli_nats: int32 [128, 8], P('batch'), may hold values from -22000 to -10001
Outputs:
- new_state: float32 [128, 64, 64, 64], P('batch', 'head')
- margin: float32 [128, 8], P('batch')
- accept: float32 [128, 8], P('batch')
All inputs are finite; a program needn't handle non-finite values.
Results may differ from a plain program's by a relative error of at most 0.0017.
Values may be sent and summed in bfloat16 or wider, within the bound.
A program may use at most 128 MiB of HBM per device.

v0:
```python
import math
import jax
import jax.numpy as jnp
from jax import lax
from jax.sharding import Mesh
from jax.sharding import PartitionSpec as P

HEAD = ("head_0", "head_1")
HEAD_BATCH = ("head_0", "head_1", "batch")


def in_blocks(x, dim, size):
    before, after = (x.shape[:dim], x.shape[dim + 1 :])
    return jnp.moveaxis(x.reshape(*before, size, -1, *after), dim, 0)


def sent_and_summed(x, axis, dim):
    size = lax.axis_size(axis)
    parts = lax.all_to_all(in_blocks(x, dim, size), axis, 0, 0, tiled=True)
    return jnp.sum(parts, axis=0)


def by_axis(x, axes):
    for axis in axes:
        x = lax.psum(x, axis)
    return x


def joined_along(parts, dim):
    parts = jnp.moveaxis(parts, 0, dim)
    shape = parts.shape
    return parts.reshape(*shape[:dim], shape[dim] * shape[dim + 1], *shape[dim + 2 :])


def sent_to_all(x, axis):
    copies = jnp.broadcast_to(x, (lax.axis_size(axis), *x.shape))
    return lax.all_to_all(copies, axis, split_axis=0, concat_axis=0, tiled=True)


def gathered_copies(x, axis, dim):
    return joined_along(sent_to_all(x, axis), dim)


def gathered_once(x, axis):
    leaves = jax.tree.leaves(x)
    sequence = sorted(range(len(leaves)), key=lambda k: -leaves[k].size)
    width = (1, *leaves[sequence[0]].shape)[-1]
    lines = [
        jnp.pad(leaves[k].reshape(-1), (0, -leaves[k].size % width)).reshape(-1, width)
        for k in sequence
    ]
    both, at, found = (sent_to_all(jnp.concatenate(lines), axis), 0, {})
    for k, line in zip(sequence, lines):
        share = both[:, at : at + len(line)].reshape(len(both), -1)
        found[k] = share[:, : leaves[k].size].reshape(-1, *leaves[k].shape)
        at += len(line)
    numbers = iter(range(len(leaves)))
    return jax.tree.map(lambda _: found[next(numbers)], x)


def combined_pairwise(pieces, combine):
    while len(jax.tree.leaves(pieces)[0]) > 1:
        pieces = jax.vmap(combine)(
            *(jax.tree.map(lambda part: part[side::2], pieces) for side in (0, 1))
        )
    return jax.tree.map(lambda part: part[0], pieces)


def combined_all(x, axis, combine):
    pieces = gathered_once(x, axis)
    return combined_pairwise(pieces, combine)


def gathered_by_type(x, axis):
    leaves, found = (jax.tree.leaves(x), {})
    for initial, a in enumerate(leaves):
        if initial not in found:
            alike = [k for k, b in enumerate(leaves) if b.dtype == a.dtype]
            got = (
                gathered_once([leaves[k] for k in alike], axis)
                if len(alike) > 1
                else [sent_to_all(a, axis)]
            )
            for k, b in zip(alike, got):
                found[k] = b
    numbers = iter(range(len(leaves)))
    return jax.tree.map(lambda _: found[next(numbers)], x)


def merged(x, axis, combine):
    pieces = gathered_by_type(x, axis)
    return combined_pairwise(pieces, combine)


def advance(start, reception_vectors, address_vectors, payload_vectors, decay, rate):
    unit = (
        address_vectors
        * lax.rsqrt(jnp.mean(address_vectors * address_vectors, -1, keepdims=True) + 1e-06)
        / math.sqrt(address_vectors.shape[-1])
    )
    inputs = tuple(
        (
            jnp.moveaxis(item, 1, 0)
            for item in (reception_vectors, address_vectors, payload_vectors, decay, unit, rate)
        )
    )

    def step(current, pieces):
        recept_now, keys_now, values_now, decay_now, unit_now, rate_now = pieces
        recall = jnp.einsum("bhij,bhj->bhi", current, unit_now, precision=lax.Precision.HIGHEST)
        current = (
            current * decay_now[:, :, None, :]
            - recall[:, :, :, None] * (unit_now * rate_now)[:, :, None, :]
            + values_now[:, :, :, None] * keys_now[:, :, None, :]
        )
        output = jnp.einsum("bhij,bhj->bhi", current, recept_now, precision=lax.Precision.HIGHEST)
        return (current, output)

    final, outputs = lax.scan(step, start, inputs)
    return (final, jnp.moveaxis(outputs, 0, 1))


def combine_stats(first, second):
    top = jnp.maximum(first[0], second[0])
    summed = first[1] * jnp.exp(first[0] - top) + second[1] * jnp.exp(second[0] - top)
    return (top, summed, first[2] + second[2])


def local_stats(logits, ids_flat, offset):
    peak = jnp.max(logits, -1)
    total = jnp.sum(jnp.exp(logits - peak[:, None]), -1)
    column = lax.broadcasted_iota(jnp.int32, logits.shape, 1)
    target = jnp.sum(jnp.where(column == (ids_flat - offset)[:, None], logits, 0.0), -1)
    return (peak, total, target)


def shards(
    incoming_hidden_stream,
    reception_projection,
    address_projection,
    payload_projection,
    sigmoid_filter_matrix,
    forgetting_speed,
    adaptation_step_size,
    diagonal_boost,
    subspace_standardize_scale,
    recurrent_memory_matrix,
    emission_projection,
    closing_standardize_scale,
    lexicon_projection,
    proposed_tokens_list,
    threshold_milli_nats,
):
    seq_dev, draft_len = proposed_tokens_list.shape
    lanes_on_shard, subspace_size = (
        recurrent_memory_matrix.shape[1],
        recurrent_memory_matrix.shape[2],
    )
    tok_dev = seq_dev * draft_len
    width = incoming_hidden_stream.shape[1]
    shape4 = (seq_dev, draft_len, lanes_on_shard, subspace_size)
    reception_vectors = jnp.dot(
        incoming_hidden_stream, reception_projection, preferred_element_type=jnp.float32
    ).reshape(shape4)
    address_vectors = jnp.dot(
        incoming_hidden_stream, address_projection, preferred_element_type=jnp.float32
    ).reshape(shape4)
    payload_vectors = jnp.dot(
        incoming_hidden_stream, payload_projection, preferred_element_type=jnp.float32
    ).reshape(shape4)
    gate = jnp.dot(
        incoming_hidden_stream, sigmoid_filter_matrix, preferred_element_type=jnp.float32
    )
    decay = jnp.exp(-forgetting_speed).reshape(shape4)
    rate = adaptation_step_size.reshape(shape4)
    new_state, wkv = advance(
        recurrent_memory_matrix, reception_vectors, address_vectors, payload_vectors, decay, rate
    )
    center = wkv - jnp.mean(wkv, -1, keepdims=True)
    interpolated_embedding = (
        center
        * lax.rsqrt(jnp.mean(center * center, -1, keepdims=True) + 1e-05)
        * subspace_standardize_scale.reshape(lanes_on_shard, subspace_size)
    )
    interpolated_embedding = (
        interpolated_embedding
        + jnp.sum(
            reception_vectors
            * address_vectors
            * diagonal_boost.reshape(lanes_on_shard, subspace_size),
            -1,
            keepdims=True,
        )
        * payload_vectors
    )
    gated = (
        interpolated_embedding.reshape(tok_dev, lanes_on_shard * subspace_size)
        * jax.nn.sigmoid(gate)
    ).astype(jnp.bfloat16)
    partial_out = jnp.dot(gated, emission_projection, preferred_element_type=jnp.float32)
    share = sent_and_summed(partial_out, HEAD, 1)
    cols = share.shape[1]
    begin = lax.axis_index(HEAD) * cols
    residual = (
        lax.dynamic_slice_in_dim(incoming_hidden_stream, begin, cols, 1).astype(jnp.float32) + share
    )
    moment_one, moment_two = (
        by_axis(jnp.sum(residual, -1), HEAD),
        by_axis(jnp.sum(residual * residual, -1), HEAD),
    )
    mean_row = moment_one / width
    variance = moment_two / width - mean_row * mean_row
    gain_part = lax.dynamic_slice_in_dim(closing_standardize_scale, begin, cols, 0)
    normed_part = (
        (residual - mean_row[:, None]) * lax.rsqrt(variance + 1e-05)[:, None] * gain_part
    ).astype(jnp.bfloat16)
    normed = gathered_copies(normed_part, HEAD, 1)
    every, every_ids = (
        lax.all_gather(normed, "batch", axis=0, tiled=True),
        lax.all_gather(proposed_tokens_list, "batch", axis=0, tiled=True),
    )
    logits = jnp.dot(every, lexicon_projection, preferred_element_type=jnp.float32)
    vcols = lexicon_projection.shape[1]
    offset = (lax.axis_index(HEAD) * lax.axis_size("batch") + lax.axis_index("batch")) * vcols
    peak, total, target = local_stats(logits, every_ids.reshape(-1), offset)
    peak, total, target = combined_all((peak, total, target), "batch", combine_stats)
    row_begin = lax.axis_index("batch") * tok_dev
    peak = lax.dynamic_slice_in_dim(peak, row_begin, tok_dev, 0)
    total = lax.dynamic_slice_in_dim(total, row_begin, tok_dev, 0)
    target = lax.dynamic_slice_in_dim(target, row_begin, tok_dev, 0)
    top, summed, target = merged((peak, total, target), HEAD, combine_stats)
    logprob = target - (top + jnp.log(summed))
    margin = logprob.reshape(seq_dev, draft_len) - threshold_milli_nats.astype(jnp.float32) / 1000.0
    accept = jnp.cumprod(jax.nn.sigmoid(margin * 0.5), axis=1)
    return (new_state, margin, accept)


def solution(mesh):
    split = Mesh(mesh.devices.reshape(4, 4, mesh.shape["batch"]), ("head_0", "head_1", "batch"))
    return jax.shard_map(
        shards,
        mesh=split,
        in_specs=(
            P("batch", None),
            P(None, HEAD),
            P(None, HEAD),
            P(None, HEAD),
            P(None, HEAD),
            P("batch", HEAD),
            P("batch", HEAD),
            P(HEAD),
            P(HEAD),
            P("batch", HEAD, None, None),
            P(HEAD, None),
            P(),
            P(None, HEAD_BATCH),
            P("batch", None),
            P("batch", None),
        ),
        out_specs=(P("batch", HEAD, None, None), P("batch", None), P("batch", None)),
        check_vma=False,
    )
```

profile of v0, /device:TPU:0, one launch (start us, length us, event | category | flops | bytes accessed | tf_op | source)
XLA Modules:
  0.0 318.9 jit_solution(11417522193714851282)
XLA Ops:
  7.2 3.3 %copy.146 = f32[16,4,64,64]{3,2,1,0:T(8,128)} copy(f32[16,4,64,64]{3,2,1,0:T(8,128)} %param.26) | data formatting | bytes 2097152
  12.3 2.0 fusion.26
  15.2 2.0 fusion.28
  18.2 2.0 multiply_reduce_fusion
  20.5 1.9 copy_bitcast_fusion.2
  22.3 1.8 reshape.126
  24.1 2.0 fusion.27
  27.0 2.0 copy_bitcast_fusion
  29.0 105.4 %while.12 = (s32[]{:T(128)}, f32[16,4,64,64]{3,2,1,0:T(8,128)}, f32[8,16,4,64]{3,2,1,0:T(4,128)S(1)}, f32[8,16,4,64]{3,2,0,1:T(4,128)}, f32[8,16,4,64]{3,2,1,0:T...) while((s32[]{:T(128)}, f32[16,4,64,64]{3,2,1,0:T(8,128)}, ...), condition=%wide.region_2.3_spmd, body=%wide.region_1.2_spmd.sunk | while | flops 7606274 | bytes 13009081 | solution.py:119
  31.5 4.9 %fusion.54 = f32[16,4,1,64]{3,2,1,0:T(1,128)S(1)} fusion(f32[16,4,64,1]{2,3,1,0:T(1,128)S(1)} %bitcast.118, f32[16,4,64,64]{3,2,1,0:T(8,128)} %get-tuple-element.245), kind=kOutput, calls=%fused_computation.79.clone.1 | convolution fusion | flops 3145728 | bytes 1081344 | tf_op jit(solution)/shard_map/while/body/eval_jaxpr/bhij,bhj->bhi/dot_general | solution.py:110
  37.2 1.5 multiply_add_fusion.8
  38.8 3.3 %fusion.55 = f32[16,4,1,64]{3,2,1,0:T(1,128)S(1)} fusion(f32[16,4,64,64]{3,2,1,0:T(8,128)S(1)} %multiply_add_fusion.8, f32[16,4,64,1]{2,3,1,0:T(1,128)S(1)} %bitcast.117), kind=kOutput, calls=%fused_computation.80.clone.1 | convolution fusion | flops 3145728 | bytes 1081344 | tf_op jit(solution)/shard_map/while/body/eval_jaxpr/bhij,bhj->bhi/dot_general | solution.py:116
  44.7 4.9 %fusion.54 = f32[16,4,1,64]{3,2,1,0:T(1,128)S(1)} fusion(f32[16,4,64,1]{2,3,1,0:T(1,128)S(1)} %bitcast.118, f32[16,4,64,64]{3,2,1,0:T(8,128)} %get-tuple-element.245), kind=kOutput, calls=%fused_computation.79.clone.1 | convolution fusion | flops 3145728 | bytes 1081344 | tf_op jit(solution)/shard_map/while/body/eval_jaxpr/bhij,bhj->bhi/dot_general | solution.py:110
  50.4 1.5 multiply_add_fusion.8
  52.0 3.3 %fusion.55 = f32[16,4,1,64]{3,2,1,0:T(1,128)S(1)} fusion(f32[16,4,64,64]{3,2,1,0:T(8,128)S(1)} %multiply_add_fusion.8, f32[16,4,64,1]{2,3,1,0:T(1,128)S(1)} %bitcast.117), kind=kOutput, calls=%fused_computation.80.clone.1 | convolution fusion | flops 3145728 | bytes 1081344 | tf_op jit(solution)/shard_map/while/body/eval_jaxpr/bhij,bhj->bhi/dot_general | solution.py:116
  57.9 4.9 %fusion.54 = f32[16,4,1,64]{3,2,1,0:T(1,128)S(1)} fusion(f32[16,4,64,1]{2,3,1,0:T(1,128)S(1)} %bitcast.118, f32[16,4,64,64]{3,2,1,0:T(8,128)} %get-tuple-element.245), kind=kOutput, calls=%fused_computation.79.clone.1 | convolution fusion | flops 3145728 | bytes 1081344 | tf_op jit(solution)/shard_map/while/body/eval_jaxpr/bhij,bhj->bhi/dot_general | solution.py:110
  63.6 1.5 multiply_add_fusion.8
  65.1 3.3 %fusion.55 = f32[16,4,1,64]{3,2,1,0:T(1,128)S(1)} fusion(f32[16,4,64,64]{3,2,1,0:T(8,128)S(1)} %multiply_add_fusion.8, f32[16,4,64,1]{2,3,1,0:T(1,128)S(1)} %bitcast.117), kind=kOutput, calls=%fused_computation.80.clone.1 | convolution fusion | flops 3145728 | bytes 1081344 | tf_op jit(solution)/shard_map/while/body/eval_jaxpr/bhij,bhj->bhi/dot_general | solution.py:116
  71.0 4.9 %fusion.54 = f32[16,4,1,64]{3,2,1,0:T(1,128)S(1)} fusion(f32[16,4,64,1]{2,3,1,0:T(1,128)S(1)} %bitcast.118, f32[16,4,64,64]{3,2,1,0:T(8,128)} %get-tuple-element.245), kind=kOutput, calls=%fused_computation.79.clone.1 | convolution fusion | flops 3145728 | bytes 1081344 | tf_op jit(solution)/shard_map/while/body/eval_jaxpr/bhij,bhj->bhi/dot_general | solution.py:110
  76.8 1.5 multiply_add_fusion.8
  78.3 3.3 %fusion.55 = f32[16,4,1,64]{3,2,1,0:T(1,128)S(1)} fusion(f32[16,4,64,64]{3,2,1,0:T(8,128)S(1)} %multiply_add_fusion.8, f32[16,4,64,1]{2,3,1,0:T(1,128)S(1)} %bitcast.117), kind=kOutput, calls=%fused_computation.80.clone.1 | convolution fusion | flops 3145728 | bytes 1081344 | tf_op jit(solution)/shard_map/while/body/eval_jaxpr/bhij,bhj->bhi/dot_general | solution.py:116
  84.2 4.9 %fusion.54 = f32[16,4,1,64]{3,2,1,0:T(1,128)S(1)} fusion(f32[16,4,64,1]{2,3,1,0:T(1,128)S(1)} %bitcast.118, f32[16,4,64,64]{3,2,1,0:T(8,128)} %get-tuple-element.245), kind=kOutput, calls=%fused_computation.79.clone.1 | convolution fusion | flops 3145728 | bytes 1081344 | tf_op jit(solution)/shard_map/while/body/eval_jaxpr/bhij,bhj->bhi/dot_general | solution.py:110
  89.9 1.5 multiply_add_fusion.8
  91.5 3.3 %fusion.55 = f32[16,4,1,64]{3,2,1,0:T(1,128)S(1)} fusion(f32[16,4,64,64]{3,2,1,0:T(8,128)S(1)} %multiply_add_fusion.8, f32[16,4,64,1]{2,3,1,0:T(1,128)S(1)} %bitcast.117), kind=kOutput, calls=%fused_computation.80.clone.1 | convolution fusion | flops 3145728 | bytes 1081344 | tf_op jit(solution)/shard_map/while/body/eval_jaxpr/bhij,bhj->bhi/dot_general | solution.py:116
  97.4 4.9 %fusion.54 = f32[16,4,1,64]{3,2,1,0:T(1,128)S(1)} fusion(f32[16,4,64,1]{2,3,1,0:T(1,128)S(1)} %bitcast.118, f32[16,4,64,64]{3,2,1,0:T(8,128)} %get-tuple-element.245), kind=kOutput, calls=%fused_computation.79.clone.1 | convolution fusion | flops 3145728 | bytes 1081344 | tf_op jit(solution)/shard_map/while/body/eval_jaxpr/bhij,bhj->bhi/dot_general | solution.py:110
  103.1 1.5 multiply_add_fusion.8
  104.7 3.3 %fusion.55 = f32[16,4,1,64]{3,2,1,0:T(1,128)S(1)} fusion(f32[16,4,64,64]{3,2,1,0:T(8,128)S(1)} %multiply_add_fusion.8, f32[16,4,64,1]{2,3,1,0:T(1,128)S(1)} %bitcast.117), kind=kOutput, calls=%fused_computation.80.clone.1 | convolution fusion | flops 3145728 | bytes 1081344 | tf_op jit(solution)/shard_map/while/body/eval_jaxpr/bhij,bhj->bhi/dot_general | solution.py:116
  110.6 4.9 %fusion.54 = f32[16,4,1,64]{3,2,1,0:T(1,128)S(1)} fusion(f32[16,4,64,1]{2,3,1,0:T(1,128)S(1)} %bitcast.118, f32[16,4,64,64]{3,2,1,0:T(8,128)} %get-tuple-element.245), kind=kOutput, calls=%fused_computation.79.clone.1 | convolution fusion | flops 3145728 | bytes 1081344 | tf_op jit(solution)/shard_map/while/body/eval_jaxpr/bhij,bhj->bhi/dot_general | solution.py:110
  116.3 1.5 multiply_add_fusion.8
  117.9 3.3 %fusion.55 = f32[16,4,1,64]{3,2,1,0:T(1,128)S(1)} fusion(f32[16,4,64,64]{3,2,1,0:T(8,128)S(1)} %multiply_add_fusion.8, f32[16,4,64,1]{2,3,1,0:T(1,128)S(1)} %bitcast.117), kind=kOutput, calls=%fused_computation.80.clone.1 | convolution fusion | flops 3145728 | bytes 1081344 | tf_op jit(solution)/shard_map/while/body/eval_jaxpr/bhij,bhj->bhi/dot_general | solution.py:116
  123.8 4.9 %fusion.54 = f32[16,4,1,64]{3,2,1,0:T(1,128)S(1)} fusion(f32[16,4,64,1]{2,3,1,0:T(1,128)S(1)} %bitcast.118, f32[16,4,64,64]{3,2,1,0:T(8,128)} %get-tuple-element.245), kind=kOutput, calls=%fused_computation.79.clone.1 | convolution fusion | flops 3145728 | bytes 1081344 | tf_op jit(solution)/shard_map/while/body/eval_jaxpr/bhij,bhj->bhi/dot_general | solution.py:110
  129.5 1.5 multiply_add_fusion.8
  131.1 3.3 %fusion.55 = f32[16,4,1,64]{3,2,1,0:T(1,128)S(1)} fusion(f32[16,4,64,64]{3,2,1,0:T(8,128)S(1)} %multiply_add_fusion.8, f32[16,4,64,1]{2,3,1,0:T(1,128)S(1)} %bitcast.117), kind=kOutput, calls=%fused_computation.80.clone.1 | convolution fusion | flops 3145728 | bytes 1081344 | tf_op jit(solution)/shard_map/while/body/eval_jaxpr/bhij,bhj->bhi/dot_general | solution.py:116
  139.9 4.2 %fusion.5 = f32[128,4096]{1,0:T(8,128)} fusion(bf16[256,4096]{1,0:T(8,128)(2,1)S(1)} %copy-done, f32[128,256]{1,0:T(8,128)S(1)} %reshape.129, bf16[128,4096]{1,0:T(8,128)(2,1)S(1)} %copy-done.3, bf16[4096,256]{1,0:T(8,128)(2,1)} %param.21), kind=kOutput, calls=%fused_computation.18 | convolution fusion | flops 537034752 | bytes 7471104 | tf_op jit(solution)/shard_map/dot_general | solution.py:200
  144.2 3.2 copy.131
  147.3 8.2 %all-to-all-start = ((f32[16,128,256]{2,1,0:T(8,128)}), f32[16,128,256]{2,1,0:T(8,128)}, u32[]{:S(2)}, u32[]{:S(2)}) async-start(f32[16,128,256]{2,1,0:T(8,128)} %bitcast.113), calls=%async_computation | async-start | bytes 4194304 | tf_op jit(solution)/shard_map/all_to_all | solution.py:19
  156.4 31.0 %all-to-all-done = f32[16,128,256]{2,1,0:T(8,128)} async-done(((f32[16,128,256]{2,1,0:T(8,128)}), f32[16,128,256]{2,1,0:T(8,128)}, u32[]{:S(2)}, u32[]{:S(2)}) %all-to-all-start) | async-done | bytes 2097184 | tf_op jit(solution)/shard_map/all_to_all | solution.py:19
  187.4 1.7 reduce_sum.85
  189.2 9.5 %all-reduce.1 = (f32[128]{0:T(128)S(1)}, f32[128]{0:T(128)S(1)}) all-reduce(f32[128]{0:T(128)S(1)} %get-tuple-element.107, f32[128]{0:T(128)S(1)} %get-tuple-element.106), channel_id=1, replica_groups=mesh['head_0'=4,'head_1'=4,'batch'=8] {'head_0'}, use_global_device_ids=true, to_apply=%region_11.12 | all-reduce | flops 256 | bytes 2048 | tf_op jit(solution)/shard_map/psum | solution.py:25
  198.7 7.7 %all-reduce = (f32[128]{0:T(128)S(1)}, f32[128]{0:T(128)S(1)}) all-reduce(f32[128]{0:T(128)S(1)} %get-tuple-element.130, f32[128]{0:T(128)S(1)} %get-tuple-element.131), channel_id=1, replica_groups=mesh['head_0'=4,'head_1'=4,'batch'=8] {'head_1'}, use_global_device_ids=true, to_apply=%region_12.13 | all-reduce | flops 256 | bytes 2048 | tf_op jit(solution)/shard_map/psum | solution.py:25
  206.9 16.6 %all_to_all.20 = bf16[16,128,256]{1,2,0:T(8,128)(2,1)} all-to-all(bf16[16,128,256]{1,2,0:T(8,128)(2,1)S(1)} %broadcast_in_dim.21), channel_id=1, replica_groups=mesh['head_0'=4,'head_1'=4,'batch'=8] {'head_0','head_1'}, dimensions={0} | all-to-all | bytes 2097152 | tf_op jit(solution)/shard_map/all_to_all | solution.py:37
  223.5 13.3 %all-gather = s32[8,16,8]{1,2,0:T(8,128)S(1)} all-gather(s32[1,16,8]{1,2,0:T(8,128)S(1)} %bitcast.136), channel_id=1, replica_groups=mesh['head_0'=4,'head_1'=4,'batch'=8] {'batch'}, dimensions={0}, use_global_device_ids=true | all-gather | bytes 4608 | tf_op jit(solution)/shard_map/all_gather | solution.py:220
  237.0 37.6 %all-gather.3.cloned.1.call-done = bf16[1024,4096]{0,1:T(8,128)(2,1)} async-done(((bf16[128,4096]{0,1:T(8,128)(2,1)}), bf16[1024,4096]{0,1:T(8,128)(2,1)}) %all-gather.3.cloned.1.call-update) | async-done | bytes 8388624 | tf_op jit(solution)/shard_map/all_gather | solution.py:219
  274.6 8.3 %fusion.23 = (f32[1024]{0:T(1024)S(1)}, f32[1024,512]{0,1:T(8,128)S(1)}) fusion(bf16[1024,4096]{0,1:T(8,128)(2,1)} %all-gather.3.cloned.1.call-done, bf16[4096,512]{1,0:T(8,128)(2,1)} %param.29), kind=kOutput, calls=%fused_computation.78 | convolution fusion | flops 4295490560 | bytes 14684160 | tf_op jit(solution)/shard_map/dot_general | solution.py:222
  284.1 4.0 %all-to-all-start.2 = ((f32[8,3,1024]{2,1,0:T(4,128)}), f32[8,3,1024]{2,1,0:T(4,128)S(1)}, u32[]{:S(2)}, u32[]{:S(2)}) async-start(f32[8,3,1024]{2,1,0:T(4,128)} %broadcast_in_dim.23), calls=%async_computation.2 | async-start | bytes 262144 | tf_op jit(solution)/shard_map/all_to_all | solution.py:37
  288.1 6.1 %all-to-all-done.2 = f32[8,3,1024]{2,1,0:T(4,128)S(1)} async-done(((f32[8,3,1024]{2,1,0:T(4,128)}), f32[8,3,1024]{2,1,0:T(4,128)S(1)}, u32[]{:S(2)}, u32[]{:S(2)}) %all-to-all-start.2) | async-done | bytes 98336 | tf_op jit(solution)/shard_map/all_to_all | solution.py:37
  295.4 6.9 %all-to-all-start.3 = ((f32[16,3,128]{2,1,0:T(4,128)}), f32[16,3,128]{2,1,0:T(4,128)S(1)}, u32[]{:S(2)}, u32[]{:S(2)}) async-start(f32[16,3,128]{2,1,0:T(4,128)} %broadcast_in_dim.25), calls=%async_computation.3 | async-start | bytes 65536 | tf_op jit(solution)/shard_map/all_to_all | solution.py:37
  302.5 7.5 %all-to-all-done.3 = f32[16,3,128]{2,1,0:T(4,128)S(1)} async-done(((f32[16,3,128]{2,1,0:T(4,128)}), f32[16,3,128]{2,1,0:T(4,128)S(1)}, u32[]{:S(2)}, u32[]{:S(2)}) %all-to-all-start.3) | async-done | bytes 24608 | tf_op jit(solution)/shard_map/all_to_all | solution.py:37
  (182 shorter events, 42.6 us)
Async XLA Ops:
  7.2 132.8 %copy-start = (bf16[256,4096]{1,0:T(8,128)(2,1)S(1)}, bf16[256,4096]{1,0:T(8,128)(2,1)}, u32[]{:S(2)}) copy-start(bf16[256,4096]{1,0:T(8,128)(2,1)} %param.27) | copy-start | bytes 6291460
  7.2 5.1 %copy-start.3 = (bf16[128,4096]{1,0:T(8,128)(2,1)S(1)}, bf16[128,4096]{1,0:T(8,128)(2,1)}, u32[]{:S(2)}) copy-start(bf16[128,4096]{1,0:T(8,128)(2,1)} %param.17) | copy-start | bytes 3145732
  14.3 3.7 %copy-start.7 = (f32[256]{0:T(256)S(1)}, f32[256]{0:T(256)}, u32[]{:S(2)}) copy-start(f32[256]{0:T(256)} %param.24) | copy-start | bytes 3076
  29.0 105.5 %copy-start.4 = (f32[16,8,4]{2,1,0:T(8,128)S(1)}, f32[16,8,4]{2,1,0:T(8,128)}, u32[]{:S(2)}) copy-start(f32[16,8,4]{2,1,0:T(8,128)} %get-tuple-element.108) | copy-start | bytes 6148
  29.0 106.1 %copy-start.8 = (f32[256]{0:T(256)S(1)}, f32[256]{0:T(256)}, u32[]{:S(2)}) copy-start(f32[256]{0:T(256)} %param.25) | copy-start | bytes 3076
  29.0 8.2 %copy-start.1 = (f32[16,4,64,64]{3,2,1,0:T(8,128)S(1)}, f32[16,4,64,64]{3,2,1,0:T(8,128)}, u32[]{:S(2)}) copy-start(f32[16,4,64,64]{3,2,1,0:T(8,128)} %get-tuple-element.245) | copy-start | bytes 3145732 | tf_op jit(solution)/shard_map/while
  38.8 3.4 %copy-start.2 = (f32[16,4,64,64]{3,2,1,0:T(8,128)}, f32[16,4,64,64]{3,2,1,0:T(8,128)S(1)}, u32[]{:S(2)}) copy-start(f32[16,4,64,64]{3,2,1,0:T(8,128)S(1)} %multiply_add_fusion.8) | copy-start | bytes 3145732 | tf_op jit(solution)/shard_map/while
  42.2 8.2 %copy-start.1 = (f32[16,4,64,64]{3,2,1,0:T(8,128)S(1)}, f32[16,4,64,64]{3,2,1,0:T(8,128)}, u32[]{:S(2)}) copy-start(f32[16,4,64,64]{3,2,1,0:T(8,128)} %get-tuple-element.245) | copy-start | bytes 3145732 | tf_op jit(solution)/shard_map/while
  51.9 3.4 %copy-start.2 = (f32[16,4,64,64]{3,2,1,0:T(8,128)}, f32[16,4,64,64]{3,2,1,0:T(8,128)S(1)}, u32[]{:S(2)}) copy-start(f32[16,4,64,64]{3,2,1,0:T(8,128)S(1)} %multiply_add_fusion.8) | copy-start | bytes 3145732 | tf_op jit(solution)/shard_map/while
  55.3 8.2 %copy-start.1 = (f32[16,4,64,64]{3,2,1,0:T(8,128)S(1)}, f32[16,4,64,64]{3,2,1,0:T(8,128)}, u32[]{:S(2)}) copy-start(f32[16,4,64,64]{3,2,1,0:T(8,128)} %get-tuple-element.245) | copy-start | bytes 3145732 | tf_op jit(solution)/shard_map/while
  65.1 3.4 %copy-start.2 = (f32[16,4,64,64]{3,2,1,0:T(8,128)}, f32[16,4,64,64]{3,2,1,0:T(8,128)S(1)}, u32[]{:S(2)}) copy-start(f32[16,4,64,64]{3,2,1,0:T(8,128)S(1)} %multiply_add_fusion.8) | copy-start | bytes 3145732 | tf_op jit(solution)/shard_map/while
  68.5 8.2 %copy-start.1 = (f32[16,4,64,64]{3,2,1,0:T(8,128)S(1)}, f32[16,4,64,64]{3,2,1,0:T(8,128)}, u32[]{:S(2)}) copy-start(f32[16,4,64,64]{3,2,1,0:T(8,128)} %get-tuple-element.245) | copy-start | bytes 3145732 | tf_op jit(solution)/shard_map/while
  78.3 3.4 %copy-start.2 = (f32[16,4,64,64]{3,2,1,0:T(8,128)}, f32[16,4,64,64]{3,2,1,0:T(8,128)S(1)}, u32[]{:S(2)}) copy-start(f32[16,4,64,64]{3,2,1,0:T(8,128)S(1)} %multiply_add_fusion.8) | copy-start | bytes 3145732 | tf_op jit(solution)/shard_map/while
  81.7 8.2 %copy-start.1 = (f32[16,4,64,64]{3,2,1,0:T(8,128)S(1)}, f32[16,4,64,64]{3,2,1,0:T(8,128)}, u32[]{:S(2)}) copy-start(f32[16,4,64,64]{3,2,1,0:T(8,128)} %get-tuple-element.245) | copy-start | bytes 3145732 | tf_op jit(solution)/shard_map/while
  91.5 3.4 %copy-start.2 = (f32[16,4,64,64]{3,2,1,0:T(8,128)}, f32[16,4,64,64]{3,2,1,0:T(8,128)S(1)}, u32[]{:S(2)}) copy-start(f32[16,4,64,64]{3,2,1,0:T(8,128)S(1)} %multiply_add_fusion.8) | copy-start | bytes 3145732 | tf_op jit(solution)/shard_map/while
  94.9 8.2 %copy-start.1 = (f32[16,4,64,64]{3,2,1,0:T(8,128)S(1)}, f32[16,4,64,64]{3,2,1,0:T(8,128)}, u32[]{:S(2)}) copy-start(f32[16,4,64,64]{3,2,1,0:T(8,128)} %get-tuple-element.245) | copy-start | bytes 3145732 | tf_op jit(solution)/shard_map/while
  104.7 3.4 %copy-start.2 = (f32[16,4,64,64]{3,2,1,0:T(8,128)}, f32[16,4,64,64]{3,2,1,0:T(8,128)S(1)}, u32[]{:S(2)}) copy-start(f32[16,4,64,64]{3,2,1,0:T(8,128)S(1)} %multiply_add_fusion.8) | copy-start | bytes 3145732 | tf_op jit(solution)/shard_map/while
  108.1 8.2 %copy-start.1 = (f32[16,4,64,64]{3,2,1,0:T(8,128)S(1)}, f32[16,4,64,64]{3,2,1,0:T(8,128)}, u32[]{:S(2)}) copy-start(f32[16,4,64,64]{3,2,1,0:T(8,128)} %get-tuple-element.245) | copy-start | bytes 3145732 | tf_op jit(solution)/shard_map/while
  117.9 3.4 %copy-start.2 = (f32[16,4,64,64]{3,2,1,0:T(8,128)}, f32[16,4,64,64]{3,2,1,0:T(8,128)S(1)}, u32[]{:S(2)}) copy-start(f32[16,4,64,64]{3,2,1,0:T(8,128)S(1)} %multiply_add_fusion.8) | copy-start | bytes 3145732 | tf_op jit(solution)/shard_map/while
  121.3 8.2 %copy-start.1 = (f32[16,4,64,64]{3,2,1,0:T(8,128)S(1)}, f32[16,4,64,64]{3,2,1,0:T(8,128)}, u32[]{:S(2)}) copy-start(f32[16,4,64,64]{3,2,1,0:T(8,128)} %get-tuple-element.245) | copy-start | bytes 3145732 | tf_op jit(solution)/shard_map/while
  131.0 3.4 %copy-start.2 = (f32[16,4,64,64]{3,2,1,0:T(8,128)}, f32[16,4,64,64]{3,2,1,0:T(8,128)S(1)}, u32[]{:S(2)}) copy-start(f32[16,4,64,64]{3,2,1,0:T(8,128)S(1)} %multiply_add_fusion.8) | copy-start | bytes 3145732 | tf_op jit(solution)/shard_map/while
  147.3 40.1 %all-to-all-start = ((f32[16,128,256]{2,1,0:T(8,128)}), f32[16,128,256]{2,1,0:T(8,128)}, u32[]{:S(2)}, u32[]{:S(2)}) async-start(f32[16,128,256]{2,1,0:T(8,128)} %bitcast.113), calls=%async_computation | async-start | bytes 4194304 | tf_op jit(solution)/shard_map/all_to_all | solution.py:19
  155.5 119.1 %all-gather.3.cloned.1.call-start = ((), (), s32[]{:S(2)}) async-start(), calls=%async_computation.4 | async-start | bytes 9437184 | tf_op jit(solution)/shard_map/all_gather | solution.py:219
  206.7 16.9 %copy-start.5 = (s32[16,8]{0,1:T(8,128)S(1)}, s32[16,8]{0,1:T(8,128)}, u32[]{:S(2)}) copy-start(s32[16,8]{0,1:T(8,128)} %param.30) | copy-start | bytes 1540
  282.9 19.5 %copy-start.6 = (s32[16,8]{0,1:T(8,128)S(1)}, s32[16,8]{0,1:T(8,128)}, u32[]{:S(2)}) copy-start(s32[16,8]{0,1:T(8,128)} %param.31) | copy-start | bytes 1540
  284.1 10.1 %all-to-all-start.2 = ((f32[8,3,1024]{2,1,0:T(4,128)}), f32[8,3,1024]{2,1,0:T(4,128)S(1)}, u32[]{:S(2)}, u32[]{:S(2)}) async-start(f32[8,3,1024]{2,1,0:T(4,128)} %broadcast_in_dim.23), calls=%async_computation.2 | async-start | bytes 262144 | tf_op jit(solution)/shard_map/all_to_all | solution.py:37
  295.4 14.6 %all-to-all-start.3 = ((f32[16,3,128]{2,1,0:T(4,128)}), f32[16,3,128]{2,1,0:T(4,128)S(1)}, u32[]{:S(2)}, u32[]{:S(2)}) async-start(f32[16,3,128]{2,1,0:T(4,128)} %broadcast_in_dim.25), calls=%async_computation.3 | async-start | bytes 65536 | tf_op jit(solution)/shard_map/all_to_all | solution.py:37
Sparse Core Ops, SparseCore 0:
  223.6 50.9 all-gather.2
where the time goes:
time: 321 us; the launch traced here: 319 us
  matrix products  84.9 us (26%)
  waiting for transfers between devices  82.3 us (26%)
  blocking collectives  47.1 us (15%)
  local copies, waits for them, and re-layouts  41.7 us (13%)
  other arithmetic  29.1 us (9%)
  starting transfers between devices  19.2 us (6%)
  between operations  14.4 us (4%)
    dot_general x8, matrix products, step(): jnp.einsum('bhij,bhj->bhi', current, unit_now, precision=lax.Precision.HI...  39.5 us
    all_gather x1, waiting for transfers between devices, shards(): lax.all_gather(normed, 'batch', axis=0, tiled=True)  37.6 us
    all_to_all x1, waiting for transfers between devices, sent_and_summed(): parts = lax.all_to_all(in_blocks(x, dim, size), axis, 0, 0, tiled=True)  31 us
    dot_general x8, matrix products, step(): jnp.einsum('bhij,bhj->bhi', current, recept_now, precision=lax.Precision....  26.8 us
    psum x2, blocking collectives, by_axis(): x = lax.psum(x, axis)  17.2 us
    all_to_all x1, blocking collectives, sent_to_all(): return lax.all_to_all(copies, axis, split_axis=0, concat_axis=0, tiled=True)  16.6 us
    all_to_all x2, waiting for transfers between devices, sent_to_all(): return lax.all_to_all(copies, axis, split_axis=0, concat_axis=0, tiled=True)  13.6 us
    all_gather x1, blocking collectives, shards(): lax.all_gather(proposed_tokens_list, 'batch', axis=0, tiled=True)  13.3 us
  transfers between devices with their start and end apart: 4, of which 4 were waited for; matrix products, arithmetic and copies ran while one was open for 0% of the time, Pallas kernels for 0%

commit v1 on v0

--- a/solution.py
+++ b/solution.py
@@ -7,6 +7,19 @@
 
 HEAD = ("head_0", "head_1")
 HEAD_BATCH = ("head_0", "head_1", "batch")
+
+
+def gather_around(x, axis, dim):
+    ways = lax.axis_size(axis)
+    up = [(d, (d + 1) % ways) for d in range(ways)]
+    down = [(d, (d - 1) % ways) for d in range(ways)]
+    earlier, later = ([x], [x])
+    for _ in range(ways // 2):
+        earlier.append(lax.ppermute(earlier[-1], axis, up))
+    for _ in range((ways - 1) // 2):
+        later.append(lax.ppermute(later[-1], axis, down))
+    line = jnp.concatenate([*earlier[::-1], *later[1:]], axis=dim)
+    return jnp.roll(line, (lax.axis_index(axis) - ways // 2) * x.shape[dim], axis=dim)
 
 
 def in_blocks(x, dim, size):
@@ -216,7 +229,7 @@
     ).astype(jnp.bfloat16)
     normed = gathered_copies(normed_part, HEAD, 1)
     every, every_ids = (
-        lax.all_gather(normed, "batch", axis=0, tiled=True),
+        gather_around(normed, "batch", 0),
         lax.all_gather(proposed_tokens_list, "batch", axis=0, tiled=True),
     )
     logits = jnp.dot(every, lexicon_projection, preferred_element_type=jnp.float32)

time: 321 us -> 340 us (1.059)
  local copies, waits for them, and re-layouts: 41.7 us -> 57.4 us
  between operations: 14.4 us -> 1.22 us
  blocking collectives: 47.1 us -> 55.1 us
  waiting for transfers between devices: 82.3 us -> 90.1 us
  starting transfers between devices: 19.2 us -> 22.9 us
  matrix products: 84.9 us -> 81.3 us
    ppermute x0 -> x7, waiting for transfers between devices: none -> 45.5 us  [the longest x4 40.4 us: gather_around(): earlier.append(lax.ppermute(earlier[-1], axis, up))]
    all_gather x1 -> x0, waiting for transfers between devices: 37.6 us -> none  [shards(): lax.all_gather(normed, 'batch', axis=0, tiled=True)]
    unnamed x21 -> x46, local copies, waits for them, and re-layouts: 4.79 us -> 20.2 us
    all_gather x1, blocking collectives: 13.3 us -> 21.4 us  [shards(): lax.all_gather(proposed_tokens_list, 'batch', axis=0, tiled=True)]
    ppermute x0 -> x7, starting transfers between devices: none -> 6.92 us  [the longest x3 6.9 us: gather_around(): later.append(lax.ppermute(later[-1], axis, down))]
    dot_general x1, matrix products: 8.27 us -> 4.66 us  [shards(): jnp.dot(every, lexicon_projection, preferred_element_type=jnp.float32)]
  transfers between devices with their start and end apart: 4 -> 10, of which waited for: 4 -> 7; matrix products, arithmetic and copies ran while one was open for 0% -> 3% of each run, Pallas kernels for 0% -> 0%
where the time goes in v1:
time: 340 us; the launch traced here: 338 us
  waiting for transfers between devices  90.1 us (26%)
  matrix products  81.3 us (24%)
  local copies, waits for them, and re-layouts  57.4 us (17%)
  blocking collectives  55.1 us (16%)
  other arithmetic  29.1 us (9%)
  starting transfers between devices  22.9 us (7%)
    ppermute x4, waiting for transfers between devices, gather_around(): earlier.append(lax.ppermute(earlier[-1], axis, up))  40.4 us
    dot_general x8, matrix products, step(): jnp.einsum('bhij,bhj->bhi', current, unit_now, precision=lax.Precision.HI...  39.5 us
    all_to_all x1, waiting for transfers between devices, sent_and_summed(): parts = lax.all_to_all(in_blocks(x, dim, size), axis, 0, 0, tiled=True)  31.1 us
    dot_general x8, matrix products, step(): jnp.einsum('bhij,bhj->bhi', current, recept_now, precision=lax.Precision....  26.8 us
    all_gather x1, blocking collectives, shards(): lax.all_gather(proposed_tokens_list, 'batch', axis=0, tiled=True)  21.4 us
    unnamed x46, local copies, waits for them, and re-layouts  20.2 us
    psum x2, blocking collectives, by_axis(): x = lax.psum(x, axis)  17.2 us
    all_to_all x1, blocking collectives, sent_to_all(): return lax.all_to_all(copies, axis, split_axis=0, concat_axis=0, tiled=True)  16.5 us
  transfers between devices with their start and end apart: 10, of which 7 were waited for; matrix products, arithmetic and copies ran while one was open for 3% of the time, Pallas kernels for 0%

profile of v1, /device:TPU:0, one launch (start us, length us, event | category | flops | bytes accessed | tf_op | source)
XLA Modules:
  0.0 337.5 jit_solution(17819999361865850470)
XLA Ops:
  0.7 3.3 copy.161
  5.8 2.0 fusion.29
  8.7 2.0 fusion.31
  11.7 2.0 multiply_reduce_fusion
  13.9 1.9 copy_bitcast_fusion.2
  15.8 1.7 reshape.126
  17.6 2.0 fusion.30
  20.5 1.9 copy_bitcast_fusion
  22.4 105.4 %while.12 = (s32[]{:T(128)}, f32[16,4,64,64]{3,2,1,0:T(8,128)}, f32[8,16,4,64]{3,2,1,0:T(4,128)S(1)}, f32[8,16,4,64]{3,2,0,1:T(4,128)}, f32[8,16,4,64]{3,2,1,0:T...) while((s32[]{:T(128)}, f32[16,4,64,64]{3,2,1,0:T(8,128)}, ...), condition=%wide.region_2.3_spmd, body=%wide.region_1.2_spmd.sunk | while | flops 7606274 | bytes 13009081 | solution.py:132
  24.9 4.9 %fusion.56 = f32[16,4,1,64]{3,2,1,0:T(1,128)S(1)} fusion(f32[16,4,64,1]{2,3,1,0:T(1,128)S(1)} %bitcast.120, f32[16,4,64,64]{3,2,1,0:T(8,128)} %get-tuple-element.245), kind=kOutput, calls=%fused_computation.98.clone.1 | convolution fusion | flops 3145728 | bytes 1081344 | tf_op jit(solution)/shard_map/while/body/eval_jaxpr/bhij,bhj->bhi/dot_general | solution.py:123
  32.2 3.3 fusion.57
  38.1 4.9 %fusion.56 = f32[16,4,1,64]{3,2,1,0:T(1,128)S(1)} fusion(f32[16,4,64,1]{2,3,1,0:T(1,128)S(1)} %bitcast.120, f32[16,4,64,64]{3,2,1,0:T(8,128)} %get-tuple-element.245), kind=kOutput, calls=%fused_computation.98.clone.1 | convolution fusion | flops 3145728 | bytes 1081344 | tf_op jit(solution)/shard_map/while/body/eval_jaxpr/bhij,bhj->bhi/dot_general | solution.py:123
  45.4 3.3 fusion.57
  51.3 4.9 %fusion.56 = f32[16,4,1,64]{3,2,1,0:T(1,128)S(1)} fusion(f32[16,4,64,1]{2,3,1,0:T(1,128)S(1)} %bitcast.120, f32[16,4,64,64]{3,2,1,0:T(8,128)} %get-tuple-element.245), kind=kOutput, calls=%fused_computation.98.clone.1 | convolution fusion | flops 3145728 | bytes 1081344 | tf_op jit(solution)/shard_map/while/body/eval_jaxpr/bhij,bhj->bhi/dot_general | solution.py:123
  58.6 3.3 fusion.57
  64.5 4.9 %fusion.56 = f32[16,4,1,64]{3,2,1,0:T(1,128)S(1)} fusion(f32[16,4,64,1]{2,3,1,0:T(1,128)S(1)} %bitcast.120, f32[16,4,64,64]{3,2,1,0:T(8,128)} %get-tuple-element.245), kind=kOutput, calls=%fused_computation.98.clone.1 | convolution fusion | flops 3145728 | bytes 1081344 | tf_op jit(solution)/shard_map/while/body/eval_jaxpr/bhij,bhj->bhi/dot_general | solution.py:123
  71.8 3.3 fusion.57
  77.7 4.9 %fusion.56 = f32[16,4,1,64]{3,2,1,0:T(1,128)S(1)} fusion(f32[16,4,64,1]{2,3,1,0:T(1,128)S(1)} %bitcast.120, f32[16,4,64,64]{3,2,1,0:T(8,128)} %get-tuple-element.245), kind=kOutput, calls=%fused_computation.98.clone.1 | convolution fusion | flops 3145728 | bytes 1081344 | tf_op jit(solution)/shard_map/while/body/eval_jaxpr/bhij,bhj->bhi/dot_general | solution.py:123
  84.9 3.3 fusion.57
  90.8 4.9 %fusion.56 = f32[16,4,1,64]{3,2,1,0:T(1,128)S(1)} fusion(f32[16,4,64,1]{2,3,1,0:T(1,128)S(1)} %bitcast.120, f32[16,4,64,64]{3,2,1,0:T(8,128)} %get-tuple-element.245), kind=kOutput, calls=%fused_computation.98.clone.1 | convolution fusion | flops 3145728 | bytes 1081344 | tf_op jit(solution)/shard_map/while/body/eval_jaxpr/bhij,bhj->bhi/dot_general | solution.py:123
  98.1 3.3 fusion.57
  104.0 4.9 %fusion.56 = f32[16,4,1,64]{3,2,1,0:T(1,128)S(1)} fusion(f32[16,4,64,1]{2,3,1,0:T(1,128)S(1)} %bitcast.120, f32[16,4,64,64]{3,2,1,0:T(8,128)} %get-tuple-element.245), kind=kOutput, calls=%fused_computation.98.clone.1 | convolution fusion | flops 3145728 | bytes 1081344 | tf_op jit(solution)/shard_map/while/body/eval_jaxpr/bhij,bhj->bhi/dot_general | solution.py:123
  111.3 3.3 fusion.57
  117.2 4.9 %fusion.56 = f32[16,4,1,64]{3,2,1,0:T(1,128)S(1)} fusion(f32[16,4,64,1]{2,3,1,0:T(1,128)S(1)} %bitcast.120, f32[16,4,64,64]{3,2,1,0:T(8,128)} %get-tuple-element.245), kind=kOutput, calls=%fused_computation.98.clone.1 | convolution fusion | flops 3145728 | bytes 1081344 | tf_op jit(solution)/shard_map/while/body/eval_jaxpr/bhij,bhj->bhi/dot_general | solution.py:123
  124.5 3.3 fusion.57
  133.3 4.2 %fusion.7 = f32[128,4096]{1,0:T(8,128)} fusion(bf16[256,4096]{1,0:T(8,128)(2,1)S(1)} %copy-done, f32[128,256]{1,0:T(8,128)S(1)} %reshape.129, bf16[128,4096]{1,0:T(8,128)(2,1)S(1)} %copy-done.3, bf16[4096,256]{1,0:T(8,128)(2,1)} %param.21), kind=kOutput, calls=%fused_computation.20 | convolution fusion | flops 537034752 | bytes 7471104 | tf_op jit(solution)/shard_map/dot_general | solution.py:213
  137.6 3.2 copy.131
  140.7 8.2 %all-to-all-start = ((f32[16,128,256]{2,1,0:T(8,128)}), f32[16,128,256]{2,1,0:T(8,128)}, u32[]{:S(2)}, u32[]{:S(2)}) async-start(f32[16,128,256]{2,1,0:T(8,128)} %bitcast.116), calls=%async_computation | async-start | bytes 4194304 | tf_op jit(solution)/shard_map/all_to_all | solution.py:32
  149.7 31.1 %all-to-all-done = f32[16,128,256]{2,1,0:T(8,128)} async-done(((f32[16,128,256]{2,1,0:T(8,128)}), f32[16,128,256]{2,1,0:T(8,128)}, u32[]{:S(2)}, u32[]{:S(2)}) %all-to-all-start) | async-done | bytes 2097184 | tf_op jit(solution)/shard_map/all_to_all | solution.py:32
  180.8 1.7 reduce_sum.85
  182.7 9.5 %all-reduce.1 = (f32[128]{0:T(128)S(1)}, f32[128]{0:T(128)S(1)}) all-reduce(f32[128]{0:T(128)S(1)} %get-tuple-element.107, f32[128]{0:T(128)S(1)} %get-tuple-element.106), channel_id=1, replica_groups=mesh['head_0'=4,'head_1'=4,'batch'=8] {'head_0'}, use_global_device_ids=true, to_apply=%region_11.12 | all-reduce | flops 256 | bytes 2048 | tf_op jit(solution)/shard_map/psum | solution.py:38
  192.1 7.7 %all-reduce = (f32[128]{0:T(128)S(1)}, f32[128]{0:T(128)S(1)}) all-reduce(f32[128]{0:T(128)S(1)} %get-tuple-element.130, f32[128]{0:T(128)S(1)} %get-tuple-element.131), channel_id=1, replica_groups=mesh['head_0'=4,'head_1'=4,'batch'=8] {'head_1'}, use_global_device_ids=true, to_apply=%region_12.13 | all-reduce | flops 256 | bytes 2048 | tf_op jit(solution)/shard_map/psum | solution.py:38
  200.3 16.5 %all_to_all.20 = bf16[16,128,256]{1,2,0:T(8,128)(2,1)S(1)} all-to-all(bf16[16,128,256]{1,2,0:T(8,128)(2,1)S(1)} %broadcast_in_dim.21), channel_id=1, replica_groups=mesh['head_0'=4,'head_1'=4,'batch'=8] {'head_0','head_1'}, dimensions={0} | all-to-all | bytes 2097152 | tf_op jit(solution)/shard_map/all_to_all | solution.py:50
  216.8 15.4 %collective-permute-done = bf16[128,4096]{0,1:T(8,128)(2,1)S(1)} collective-permute-done((bf16[128,4096]{0,1:T(8,128)(2,1)S(1)}, bf16[128,4096]{0,1:T(8,128)(2,1)S(1)}, u32[]{:S(2)}, u32[]{:S(2)}) %collective-permute-start) | collective-permute-done | bytes 1048608 | tf_op jit(solution)/shard_map/ppermute | solution.py:18
  232.3 3.0 collective-permute-start.4
  235.2 12.5 %collective-permute-done.1 = bf16[128,4096]{0,1:T(8,128)(2,1)S(1)} collective-permute-done((bf16[128,4096]{0,1:T(8,128)(2,1)S(1)}, bf16[128,4096]{0,1:T(8,128)(2,1)S(1)}, u32[]{:S(2)}, u32[]{:S(2)}) %collective-permute-start.1) | collective-permute-done | bytes 1048608 | tf_op jit(solution)/shard_map/ppermute | solution.py:18
  247.7 3.0 collective-permute-start.5
  250.8 12.5 %collective-permute-done.2 = bf16[128,4096]{0,1:T(8,128)(2,1)} collective-permute-done((bf16[128,4096]{0,1:T(8,128)(2,1)S(1)}, bf16[128,4096]{0,1:T(8,128)(2,1)}, u32[]{:S(2)}, u32[]{:S(2)}) %collective-permute-start.2) | collective-permute-done | bytes 1048608 | tf_op jit(solution)/shard_map/ppermute | solution.py:18
  263.2 21.4 %all-gather = s32[8,16,8]{1,2,0:T(8,128)S(1)} all-gather(s32[1,16,8]{1,2,0:T(8,128)S(1)} %bitcast.138), channel_id=1, replica_groups=mesh['head_0'=4,'head_1'=4,'batch'=8] {'batch'}, dimensions={0}, use_global_device_ids=true | all-gather | bytes 4608 | tf_op jit(solution)/shard_map/all_gather | solution.py:233
  287.3 1.7 constant_dynamic-update-slice_fusion.15
  290.1 1.6 constant_dynamic-update-slice_fusion.11
  293.3 5.1 %collective-permute-done.6 = bf16[128,4096]{0,1:T(8,128)(2,1)S(1)} collective-permute-done((bf16[128,4096]{0,1:T(8,128)(2,1)}, bf16[128,4096]{0,1:T(8,128)(2,1)S(1)}, u32[]{:S(2)}, u32[]{:S(2)}) %collective-permute-start.6) | collective-permute-done | bytes 1048608 | tf_op jit(solution)/shard_map/ppermute | solution.py:20
  303.1 1.7 constant_dynamic-update-slice_fusion.3
  306.8 4.7 %fusion.26 = (f32[1024]{0:T(1024)S(1)}, f32[1024,512]{0,1:T(8,128)S(1)}) fusion(bf16[4096,512]{1,0:T(8,128)(2,1)S(1)} %copy-done.13, bf16[2048,4096]{0,1:T(8,128)(2,1)S(1)} %constant_dynamic-update-slice_fusion.1, s32[]{:T(128)S(6)} %select_n.28), kind=kOutput, calls=%fused_computation.97 | convolution fusion | flops 4295490560 | bytes 14684164 | tf_op jit(solution)/shard_map/dot_general | solution.py:235
  312.8 4.3 %all-to-all-start.2 = ((f32[8,3,1024]{2,1,0:T(4,128)}), f32[8,3,1024]{2,1,0:T(4,128)S(1)}, u32[]{:S(2)}, u32[]{:S(2)}) async-start(f32[8,3,1024]{2,1,0:T(4,128)} %broadcast_in_dim.23), calls=%async_computation.2 | async-start | bytes 262144 | tf_op jit(solution)/shard_map/all_to_all | solution.py:50
  317.1 6.1 %all-to-all-done.2 = f32[8,3,1024]{2,1,0:T(4,128)S(1)} async-done(((f32[8,3,1024]{2,1,0:T(4,128)}), f32[8,3,1024]{2,1,0:T(4,128)S(1)}, u32[]{:S(2)}, u32[]{:S(2)}) %all-to-all-start.2) | async-done | bytes 98336 | tf_op jit(solution)/shard_map/all_to_all | solution.py:50
  324.4 3.5 %all-to-all-start.3 = ((f32[16,3,128]{2,1,0:T(4,128)}), f32[16,3,128]{2,1,0:T(4,128)S(1)}, u32[]{:S(2)}, u32[]{:S(2)}) async-start(f32[16,3,128]{2,1,0:T(4,128)} %broadcast_in_dim.25), calls=%async_computation.3 | async-start | bytes 65536 | tf_op jit(solution)/shard_map/all_to_all | solution.py:50
  328.0 7.5 %all-to-all-done.3 = f32[16,3,128]{2,1,0:T(4,128)S(1)} async-done(((f32[16,3,128]{2,1,0:T(4,128)}), f32[16,3,128]{2,1,0:T(4,128)S(1)}, u32[]{:S(2)}, u32[]{:S(2)}) %all-to-all-start.3) | async-done | bytes 24608 | tf_op jit(solution)/shard_map/all_to_all | solution.py:50
  (219 shorter events, 66.6 us)
Async XLA Ops:
  0.6 132.7 %copy-start = (bf16[256,4096]{1,0:T(8,128)(2,1)S(1)}, bf16[256,4096]{1,0:T(8,128)(2,1)}, u32[]{:S(2)}) copy-start(bf16[256,4096]{1,0:T(8,128)(2,1)} %param.27) | copy-start | bytes 6291460
  0.6 5.1 %copy-start.3 = (bf16[128,4096]{1,0:T(8,128)(2,1)S(1)}, bf16[128,4096]{1,0:T(8,128)(2,1)}, u32[]{:S(2)}) copy-start(bf16[128,4096]{1,0:T(8,128)(2,1)} %param.17) | copy-start | bytes 3145732
  7.8 3.8 %copy-start.11 = (f32[256]{0:T(256)S(1)}, f32[256]{0:T(256)}, u32[]{:S(2)}) copy-start(f32[256]{0:T(256)} %param.24) | copy-start | bytes 3076
  22.4 105.5 %copy-start.8 = (f32[16,8,4]{2,1,0:T(8,128)S(1)}, f32[16,8,4]{2,1,0:T(8,128)}, u32[]{:S(2)}) copy-start(f32[16,8,4]{2,1,0:T(8,128)} %get-tuple-element.108) | copy-start | bytes 6148
  22.4 106.1 %copy-start.12 = (f32[256]{0:T(256)S(1)}, f32[256]{0:T(256)}, u32[]{:S(2)}) copy-start(f32[256]{0:T(256)} %param.25) | copy-start | bytes 3076
  22.4 8.2 %copy-start.1 = (f32[16,4,64,64]{3,2,1,0:T(8,128)S(1)}, f32[16,4,64,64]{3,2,1,0:T(8,128)}, u32[]{:S(2)}) copy-start(f32[16,4,64,64]{3,2,1,0:T(8,128)} %get-tuple-element.245) | copy-start | bytes 3145732 | tf_op jit(solution)/shard_map/while
  32.2 3.4 %copy-start.2 = (f32[16,4,64,64]{3,2,1,0:T(8,128)}, f32[16,4,64,64]{3,2,1,0:T(8,128)S(1)}, u32[]{:S(2)}) copy-start(f32[16,4,64,64]{3,2,1,0:T(8,128)S(1)} %multiply_add_fusion.8) | copy-start | bytes 3145732 | tf_op jit(solution)/shard_map/while
  35.6 8.2 %copy-start.1 = (f32[16,4,64,64]{3,2,1,0:T(8,128)S(1)}, f32[16,4,64,64]{3,2,1,0:T(8,128)}, u32[]{:S(2)}) copy-start(f32[16,4,64,64]{3,2,1,0:T(8,128)} %get-tuple-element.245) | copy-start | bytes 3145732 | tf_op jit(solution)/shard_map/while
  45.4 3.4 %copy-start.2 = (f32[16,4,64,64]{3,2,1,0:T(8,128)}, f32[16,4,64,64]{3,2,1,0:T(8,128)S(1)}, u32[]{:S(2)}) copy-start(f32[16,4,64,64]{3,2,1,0:T(8,128)S(1)} %multiply_add_fusion.8) | copy-start | bytes 3145732 | tf_op jit(solution)/shard_map/while
  48.8 8.2 %copy-start.1 = (f32[16,4,64,64]{3,2,1,0:T(8,128)S(1)}, f32[16,4,64,64]{3,2,1,0:T(8,128)}, u32[]{:S(2)}) copy-start(f32[16,4,64,64]{3,2,1,0:T(8,128)} %get-tuple-element.245) | copy-start | bytes 3145732 | tf_op jit(solution)/shard_map/while
  58.6 3.4 %copy-start.2 = (f32[16,4,64,64]{3,2,1,0:T(8,128)}, f32[16,4,64,64]{3,2,1,0:T(8,128)S(1)}, u32[]{:S(2)}) copy-start(f32[16,4,64,64]{3,2,1,0:T(8,128)S(1)} %multiply_add_fusion.8) | copy-start | bytes 3145732 | tf_op jit(solution)/shard_map/while
  62.0 8.2 %copy-start.1 = (f32[16,4,64,64]{3,2,1,0:T(8,128)S(1)}, f32[16,4,64,64]{3,2,1,0:T(8,128)}, u32[]{:S(2)}) copy-start(f32[16,4,64,64]{3,2,1,0:T(8,128)} %get-tuple-element.245) | copy-start | bytes 3145732 | tf_op jit(solution)/shard_map/while
  71.7 3.4 %copy-start.2 = (f32[16,4,64,64]{3,2,1,0:T(8,128)}, f32[16,4,64,64]{3,2,1,0:T(8,128)S(1)}, u32[]{:S(2)}) copy-start(f32[16,4,64,64]{3,2,1,0:T(8,128)S(1)} %multiply_add_fusion.8) | copy-start | bytes 3145732 | tf_op jit(solution)/shard_map/while
  75.1 8.2 %copy-start.1 = (f32[16,4,64,64]{3,2,1,0:T(8,128)S(1)}, f32[16,4,64,64]{3,2,1,0:T(8,128)}, u32[]{:S(2)}) copy-start(f32[16,4,64,64]{3,2,1,0:T(8,128)} %get-tuple-element.245) | copy-start | bytes 3145732 | tf_op jit(solution)/shard_map/while
  84.9 3.4 %copy-start.2 = (f32[16,4,64,64]{3,2,1,0:T(8,128)}, f32[16,4,64,64]{3,2,1,0:T(8,128)S(1)}, u32[]{:S(2)}) copy-start(f32[16,4,64,64]{3,2,1,0:T(8,128)S(1)} %multiply_add_fusion.8) | copy-start | bytes 3145732 | tf_op jit(solution)/shard_map/while
  88.3 8.2 %copy-start.1 = (f32[16,4,64,64]{3,2,1,0:T(8,128)S(1)}, f32[16,4,64,64]{3,2,1,0:T(8,128)}, u32[]{:S(2)}) copy-start(f32[16,4,64,64]{3,2,1,0:T(8,128)} %get-tuple-element.245) | copy-start | bytes 3145732 | tf_op jit(solution)/shard_map/while
  98.1 3.4 %copy-start.2 = (f32[16,4,64,64]{3,2,1,0:T(8,128)}, f32[16,4,64,64]{3,2,1,0:T(8,128)S(1)}, u32[]{:S(2)}) copy-start(f32[16,4,64,64]{3,2,1,0:T(8,128)S(1)} %multiply_add_fusion.8) | copy-start | bytes 3145732 | tf_op jit(solution)/shard_map/while
  101.5 8.2 %copy-start.1 = (f32[16,4,64,64]{3,2,1,0:T(8,128)S(1)}, f32[16,4,64,64]{3,2,1,0:T(8,128)}, u32[]{:S(2)}) copy-start(f32[16,4,64,64]{3,2,1,0:T(8,128)} %get-tuple-element.245) | copy-start | bytes 3145732 | tf_op jit(solution)/shard_map/while
  111.3 3.4 %copy-start.2 = (f32[16,4,64,64]{3,2,1,0:T(8,128)}, f32[16,4,64,64]{3,2,1,0:T(8,128)S(1)}, u32[]{:S(2)}) copy-start(f32[16,4,64,64]{3,2,1,0:T(8,128)S(1)} %multiply_add_fusion.8) | copy-start | bytes 3145732 | tf_op jit(solution)/shard_map/while
  114.7 8.2 %copy-start.1 = (f32[16,4,64,64]{3,2,1,0:T(8,128)S(1)}, f32[16,4,64,64]{3,2,1,0:T(8,128)}, u32[]{:S(2)}) copy-start(f32[16,4,64,64]{3,2,1,0:T(8,128)} %get-tuple-element.245) | copy-start | bytes 3145732 | tf_op jit(solution)/shard_map/while
  124.5 3.4 %copy-start.2 = (f32[16,4,64,64]{3,2,1,0:T(8,128)}, f32[16,4,64,64]{3,2,1,0:T(8,128)S(1)}, u32[]{:S(2)}) copy-start(f32[16,4,64,64]{3,2,1,0:T(8,128)S(1)} %multiply_add_fusion.8) | copy-start | bytes 3145732 | tf_op jit(solution)/shard_map/while
  140.7 40.0 %all-to-all-start = ((f32[16,128,256]{2,1,0:T(8,128)}), f32[16,128,256]{2,1,0:T(8,128)}, u32[]{:S(2)}, u32[]{:S(2)}) async-start(f32[16,128,256]{2,1,0:T(8,128)} %bitcast.116), calls=%async_computation | async-start | bytes 4194304 | tf_op jit(solution)/shard_map/all_to_all | solution.py:32
  182.5 80.7 %copy-start.9 = (s32[16,8]{0,1:T(8,128)S(1)}, s32[16,8]{0,1:T(8,128)}, u32[]{:S(2)}) copy-start(s32[16,8]{0,1:T(8,128)} %param.30) | copy-start | bytes 1540
  216.8 15.4 %collective-permute-start = (bf16[128,4096]{0,1:T(8,128)(2,1)S(1)}, bf16[128,4096]{0,1:T(8,128)(2,1)S(1)}, u32[]{:S(2)}, u32[]{:S(2)}) collective-permute-start(bf16[128,4096]{0,1:T(8,128)(2,1)S(1)} %bitcast.111), channel_id=1, source_target_pairs={{0,1},{1,2},{2,3},{3,4},{4,5},{5,6},{6,7},{7,0},{8,9},{9,10},{10,1... | collective-permute-start | bytes 3145736 | tf_op jit(solution)/shard_map/ppermute | solution.py:18
  232.2 15.5 %copy-start.4 = (bf16[128,4096]{0,1:T(8,128)(2,1)}, bf16[128,4096]{0,1:T(8,128)(2,1)S(1)}, u32[]{:S(2)}) copy-start(bf16[128,4096]{0,1:T(8,128)(2,1)S(1)} %collective-permute-done) | copy-start | bytes 3145732
  232.2 15.4 %collective-permute-start.1 = (bf16[128,4096]{0,1:T(8,128)(2,1)S(1)}, bf16[128,4096]{0,1:T(8,128)(2,1)S(1)}, u32[]{:S(2)}, u32[]{:S(2)}) collective-permute-start(bf16[128,4096]{0,1:T(8,128)(2,1)S(1)} %collective-permute-done), channel_id=1, source_target_pairs={{0,1},{1,2},{2,3},{3,4},{4,5},{5,6},{6,7},{7,0},{8,9},{9,10},{10,1... | collective-permute-start | bytes 3145736 | tf_op jit(solution)/shard_map/ppermute | solution.py:18
  232.3 15.4 %collective-permute-start.4 = (bf16[128,4096]{0,1:T(8,128)(2,1)S(1)}, bf16[128,4096]{0,1:T(8,128)(2,1)}, u32[]{:S(2)}, u32[]{:S(2)}) collective-permute-start(bf16[128,4096]{0,1:T(8,128)(2,1)S(1)} %bitcast.112), channel_id=1, source_target_pairs={{0,7},{1,0},{2,1},{3,2},{4,3},{5,4},{6,5},{7,6},{8,15},{9,8},{10,9... | collective-permute-start | bytes 3145736 | tf_op jit(solution)/shard_map/ppermute | solution.py:20
  247.7 3.1 copy-start.6
  247.7 15.5 %collective-permute-start.2 = (bf16[128,4096]{0,1:T(8,128)(2,1)S(1)}, bf16[128,4096]{0,1:T(8,128)(2,1)}, u32[]{:S(2)}, u32[]{:S(2)}) collective-permute-start(bf16[128,4096]{0,1:T(8,128)(2,1)S(1)} %collective-permute-done.1), channel_id=1, source_target_pairs={{0,1},{1,2},{2,3},{3,4},{4,5},{5,6},{6,7},{7,0},{8,9},{9,10},{10,1... | collective-permute-start | bytes 3145736 | tf_op jit(solution)/shard_map/ppermute | solution.py:18
  247.7 37.2 %collective-permute-start.5 = (bf16[128,4096]{0,1:T(8,128)(2,1)}, bf16[128,4096]{0,1:T(8,128)(2,1)}, u32[]{:S(2)}, u32[]{:S(2)}) collective-permute-start(bf16[128,4096]{0,1:T(8,128)(2,1)} %collective-permute-done.4), channel_id=1, source_target_pairs={{0,7},{1,0},{2,1},{3,2},{4,3},{5,4},{6,5},{7,6},{8,15},{9,8},{10,9... | collective-permute-start | bytes 3145736 | tf_op jit(solution)/shard_map/ppermute | solution.py:20
  263.2 22.6 %collective-permute-start.3 = (bf16[128,4096]{0,1:T(8,128)(2,1)}, bf16[128,4096]{0,1:T(8,128)(2,1)}, u32[]{:S(2)}, u32[]{:S(2)}) collective-permute-start(bf16[128,4096]{0,1:T(8,128)(2,1)} %collective-permute-done.2), channel_id=1, source_target_pairs={{0,1},{1,2},{2,3},{3,4},{4,5},{5,6},{6,7},{7,0},{8,9},{9,10},{10,1... | collective-permute-start | bytes 3145736 | tf_op jit(solution)/shard_map/ppermute | solution.py:18
  284.9 4.2 %copy-start.7 = (bf16[128,4096]{0,1:T(8,128)(2,1)S(1)}, bf16[128,4096]{0,1:T(8,128)(2,1)}, u32[]{:S(2)}) copy-start(bf16[128,4096]{0,1:T(8,128)(2,1)} %copy-done.6) | copy-start | bytes 3145732
  284.9 13.5 %collective-permute-start.6 = (bf16[128,4096]{0,1:T(8,128)(2,1)}, bf16[128,4096]{0,1:T(8,128)(2,1)S(1)}, u32[]{:S(2)}, u32[]{:S(2)}) collective-permute-start(bf16[128,4096]{0,1:T(8,128)(2,1)} %collective-permute-done.5), channel_id=1, source_target_pairs={{0,7},{1,0},{2,1},{3,2},{4,3},{5,4},{6,5},{7,6},{8,15},{9,8},{10,9... | collective-permute-start | bytes 3145736 | tf_op jit(solution)/shard_map/ppermute | solution.py:20
  287.3 2.1 copy-start.5
  303.1 3.7 %copy-start.13 = (bf16[4096,512]{1,0:T(8,128)(2,1)S(1)}, bf16[4096,512]{1,0:T(8,128)(2,1)}, u32[]{:S(2)}) copy-start(bf16[4096,512]{1,0:T(8,128)(2,1)} %param.29) | copy-start | bytes 12582916
  311.5 16.4 %copy-start.10 = (s32[16,8]{0,1:T(8,128)S(1)}, s32[16,8]{0,1:T(8,128)}, u32[]{:S(2)}) copy-start(s32[16,8]{0,1:T(8,128)} %param.31) | copy-start | bytes 1540
  312.8 10.4 %all-to-all-start.2 = ((f32[8,3,1024]{2,1,0:T(4,128)}), f32[8,3,1024]{2,1,0:T(4,128)S(1)}, u32[]{:S(2)}, u32[]{:S(2)}) async-start(f32[8,3,1024]{2,1,0:T(4,128)} %broadcast_in_dim.23), calls=%async_computation.2 | async-start | bytes 262144 | tf_op jit(solution)/shard_map/all_to_all | solution.py:50
  324.4 11.0 %all-to-all-start.3 = ((f32[16,3,128]{2,1,0:T(4,128)}), f32[16,3,128]{2,1,0:T(4,128)S(1)}, u32[]{:S(2)}, u32[]{:S(2)}) async-start(f32[16,3,128]{2,1,0:T(4,128)} %broadcast_in_dim.25), calls=%async_computation.3 | async-start | bytes 65536 | tf_op jit(solution)/shard_map/all_to_all | solution.py:50
